TPU v7x, 16 devices: a 4x2x1 block of a 4x4x8 slice. The times are simulated.
16 devices in a mesh: dp: 2 (over y, z), pp: 8 (over x, core).
Axes of the slice: x: 4, y: 2, z: 1, core: 2. Of those that a mesh axis runs over, the one named last changes fastest.
The devices are a block of a 4x4x8 slice.
Arguments:
- acts_in: bfloat16 [16, 8, 192, 768], P(None, 'dp'), parts along dimension 1
- cotangent: bfloat16 [16, 8, 192, 768], P(None, 'dp'), parts along dimension 1
- ln1_gain: bfloat16 [8, 768], P('pp')
- ln1_shift: bfloat16 [8, 768], P('pp')
- w_qkv: bfloat16 [8, 768, 2304], P('pp')
- b_qkv: bfloat16 [8, 2304], P('pp')
- w_proj: bfloat16 [8, 12, 64, 768], P('pp')
- b_proj: bfloat16 [8, 768], P('pp')
- ln2_gain: bfloat16 [8, 768], P('pp')
- ln2_shift: bfloat16 [8, 768], P('pp')
- w_up: bfloat16 [8, 768, 3072], P('pp')
- b_up: bfloat16 [8, 3072], P('pp')
- w_down: bfloat16 [8, 3072, 768], P('pp')
- b_down: bfloat16 [8, 768], P('pp')
Outputs:
- output 1: bfloat16 [16, 8, 192, 768], P(None, 'dp'), parts along dimension 1
- output 2: bfloat16 [16, 8, 192, 768], P(None, 'dp'), parts along dimension 1
- output 3: float32 [16, 768], P(('dp', 'pp')), parts along dimension 0
- output 4: float32 [16, 768], P(('dp', 'pp')), parts along dimension 0
- output 5: float32 [16, 768, 2304], P(('dp', 'pp')), parts along dimension 0
- output 6: float32 [16, 2304], P(('dp', 'pp')), parts along dimension 0
- output 7: float32 [16, 12, 64, 768], P(('dp', 'pp')), parts along dimension 0
- output 8: float32 [16, 768], P(('dp', 'pp')), parts along dimension 0
- output 9: float32 [16, 768], P(('dp', 'pp')), parts along dimension 0
- output 10: float32 [16, 768], P(('dp', 'pp')), parts along dimension 0
- output 11: float32 [16, 768, 3072], P(('dp', 'pp')), parts along dimension 0
- output 12: float32 [16, 3072], P(('dp', 'pp')), parts along dimension 0
- output 13: float32 [16, 3072, 768], P(('dp', 'pp')), parts along dimension 0
- output 14: float32 [16, 768], P(('dp', 'pp')), parts along dimension 0
There are 2 independent parts. A program takes and returns all parts, laid end to end along the dimension named above; an argument that names none is the same for every part.
All inputs are finite; a program needn't handle non-finite values.
Results may differ from a plain program's by a relative error of at most 0.02.
Values are sent between devices in bfloat16 or wider.
A program may use at most 768 MiB of HBM per device.

v0:
```python
import jax
import jax.numpy as jnp
from jax import lax
from jax.sharding import PartitionSpec as P

LN_EPS = 1e-5
PARAM_RANKS = (2, 2, 3, 2, 4, 2, 2, 2, 3, 2, 3, 2)


def layer_norm(x_wide, gain, shift):
    mean_val = jnp.mean(x_wide, axis=-1, keepdims=True)
    centered = x_wide - mean_val
    variance = jnp.mean(centered * centered, axis=-1, keepdims=True)
    return centered * lax.rsqrt(variance + LN_EPS) * gain + shift


def gelu_tanh(pre_act):
    return jax.nn.gelu(pre_act, approximate=True)


def layer_forward(weights, x_act):
    g_one, s_one, w_qkv, b_qkv, w_proj, b_proj, g_two, s_two, w_up, b_up, w_down, b_down = weights
    n_batch, n_seq = x_act.shape[0], x_act.shape[1]
    n_heads, head_dim = w_proj.shape[0], w_proj.shape[1]
    x_wide = x_act.astype(jnp.float32)
    h_one = layer_norm(x_wide, g_one.astype(jnp.float32), s_one.astype(jnp.float32)).astype(jnp.bfloat16)
    qkv_act = (jnp.einsum('bsd,de->bse', h_one, w_qkv, preferred_element_type=jnp.float32) + b_qkv.astype(jnp.float32)).astype(jnp.bfloat16)
    qkv_heads = qkv_act.reshape(n_batch, n_seq, 3, n_heads, head_dim)
    scores = jnp.einsum('bqhd,bkhd->bhqk', qkv_heads[:, :, 0], qkv_heads[:, :, 1], preferred_element_type=jnp.float32) * (head_dim ** -0.5)
    causal = jnp.arange(n_seq)[:, None] >= jnp.arange(n_seq)[None, :]
    attn_probs = jax.nn.softmax(jnp.where(causal, scores, -1e30), axis=-1).astype(jnp.bfloat16)
    attn_mix = jnp.einsum('bhqk,bkhd->bqhd', attn_probs, qkv_heads[:, :, 2], preferred_element_type=jnp.float32).astype(jnp.bfloat16)
    x_mid = (x_wide + jnp.einsum('bqhd,hde->bqe', attn_mix, w_proj, preferred_element_type=jnp.float32) + b_proj.astype(jnp.float32)).astype(jnp.bfloat16)
    mid_wide = x_mid.astype(jnp.float32)
    h_two = layer_norm(mid_wide, g_two.astype(jnp.float32), s_two.astype(jnp.float32)).astype(jnp.bfloat16)
    pre_act = jnp.einsum('bsd,df->bsf', h_two, w_up, preferred_element_type=jnp.float32) + b_up.astype(jnp.float32)
    hidden = gelu_tanh(pre_act).astype(jnp.bfloat16)
    y_act = (mid_wide + jnp.einsum('bsf,fd->bsd', hidden, w_down, preferred_element_type=jnp.float32) + b_down.astype(jnp.float32)).astype(jnp.bfloat16)
    return y_act, (x_act, qkv_act, attn_probs, attn_mix, x_mid, pre_act)


def layer_backward(weights, saved, grad_y):
    g_one, s_one, w_qkv, b_qkv, w_proj, b_proj, g_two, s_two, w_up, b_up, w_down, b_down = weights
    x_act, qkv_act, attn_probs, attn_mix, x_mid, pre_act = saved
    n_batch, n_seq = x_act.shape[0], x_act.shape[1]
    n_heads, head_dim = w_proj.shape[0], w_proj.shape[1]
    grad_wide = grad_y.astype(jnp.float32)
    hidden_f, gelu_pull = jax.vjp(gelu_tanh, pre_act)
    grad_w_down = jnp.einsum('bsf,bsd->fd', hidden_f.astype(jnp.bfloat16), grad_y, preferred_element_type=jnp.float32)
    grad_b_down = jnp.sum(grad_wide, axis=(0, 1))
    grad_hidden = jnp.einsum('bsd,fd->bsf', grad_y, w_down, preferred_element_type=jnp.float32).astype(jnp.bfloat16)
    grad_pre = gelu_pull(grad_hidden.astype(jnp.float32))[0]
    grad_b_up = jnp.sum(grad_pre, axis=(0, 1))
    grad_pre_bf = grad_pre.astype(jnp.bfloat16)
    h_two_f, ln_two_pull = jax.vjp(layer_norm, x_mid.astype(jnp.float32), g_two.astype(jnp.float32), s_two.astype(jnp.float32))
    grad_w_up = jnp.einsum('bsd,bsf->df', h_two_f.astype(jnp.bfloat16), grad_pre_bf, preferred_element_type=jnp.float32)
    grad_h_two = jnp.einsum('bsf,df->bsd', grad_pre_bf, w_up, preferred_element_type=jnp.float32).astype(jnp.bfloat16)
    grad_mid_ln, grad_g_two, grad_s_two = ln_two_pull(grad_h_two.astype(jnp.float32))
    grad_mid = (grad_wide + grad_mid_ln).astype(jnp.bfloat16)
    grad_mid_wide = grad_mid.astype(jnp.float32)
    grad_b_proj = jnp.sum(grad_mid_wide, axis=(0, 1))
    grad_w_proj = jnp.einsum('bqhd,bqe->hde', attn_mix, grad_mid, preferred_element_type=jnp.float32)
    grad_mix = jnp.einsum('bqe,hde->bqhd', grad_mid, w_proj, preferred_element_type=jnp.float32).astype(jnp.bfloat16)
    qkv_heads = qkv_act.reshape(n_batch, n_seq, 3, n_heads, head_dim)
    grad_probs = jnp.einsum('bqhd,bkhd->bhqk', grad_mix, qkv_heads[:, :, 2], preferred_element_type=jnp.float32).astype(jnp.bfloat16).astype(jnp.float32)
    grad_v = jnp.einsum('bhqk,bqhd->bkhd', attn_probs, grad_mix, preferred_element_type=jnp.float32)
    probs_wide = attn_probs.astype(jnp.float32)
    row_dot = jnp.sum(grad_probs * probs_wide, axis=-1, keepdims=True)
    grad_scores = (probs_wide * (grad_probs - row_dot) * (head_dim ** -0.5)).astype(jnp.bfloat16)
    grad_q = jnp.einsum('bhqk,bkhd->bqhd', grad_scores, qkv_heads[:, :, 1], preferred_element_type=jnp.float32)
    grad_k = jnp.einsum('bhqk,bqhd->bkhd', grad_scores, qkv_heads[:, :, 0], preferred_element_type=jnp.float32)
    grad_qkv = jnp.stack([grad_q.astype(jnp.bfloat16), grad_k.astype(jnp.bfloat16), grad_v.astype(jnp.bfloat16)], axis=2).reshape(qkv_act.shape)
    grad_b_qkv = jnp.sum(grad_qkv, axis=(0, 1), dtype=jnp.float32)
    h_one_f, ln_one_pull = jax.vjp(layer_norm, x_act.astype(jnp.float32), g_one.astype(jnp.float32), s_one.astype(jnp.float32))
    grad_w_qkv = jnp.einsum('bsd,bse->de', h_one_f.astype(jnp.bfloat16), grad_qkv, preferred_element_type=jnp.float32)
    grad_h_one = jnp.einsum('bse,de->bsd', grad_qkv, w_qkv, preferred_element_type=jnp.float32).astype(jnp.bfloat16)
    grad_x_ln, grad_g_one, grad_s_one = ln_one_pull(grad_h_one.astype(jnp.float32))
    grad_x = (grad_mid_wide + grad_x_ln).astype(jnp.bfloat16)
    return grad_x, (grad_g_one, grad_s_one, grad_w_qkv, grad_b_qkv, grad_w_proj, grad_b_proj, grad_g_two, grad_s_two, grad_w_up, grad_b_up, grad_w_down, grad_b_down)


def solution(mesh):
    n_stages = mesh.shape['pp']
    last_stage = n_stages - 1
    fwd_pairs = [(source, source + 1) for source in range(n_stages - 1)]
    bwd_pairs = [(source + 1, source) for source in range(n_stages - 1)]
    act_spec = P(None, 'dp', None, None)
    param_specs = tuple(P(*(('pp',) + (None,) * (rank_n - 1))) for rank_n in PARAM_RANKS)
    grad_specs = tuple(P(*((('dp', 'pp'),) + (None,) * (rank_n - 1))) for rank_n in PARAM_RANKS)

    def stage_body(acts_in, cotangent, *stacked_w):
        weights = tuple(tensor[0] for tensor in stacked_w)
        stage_idx = lax.axis_index('pp')
        n_micro, n_rows, n_seq, n_width = acts_in.shape
        n_heads, head_dim = stacked_w[4].shape[1], stacked_w[4].shape[2]
        n_hidden = stacked_w[8].shape[2]
        mb_shape = (n_rows, n_seq, n_width)
        n_steps = n_micro + n_stages - 1
        saved_init = (
            jnp.zeros((n_micro, n_rows, n_seq, n_width), jnp.bfloat16),
            jnp.zeros((n_micro, n_rows, n_seq, 3 * n_width), jnp.bfloat16),
            jnp.zeros((n_micro, n_rows, n_heads, n_seq, n_seq), jnp.bfloat16),
            jnp.zeros((n_micro, n_rows, n_seq, n_heads, head_dim), jnp.bfloat16),
            jnp.zeros((n_micro, n_rows, n_seq, n_width), jnp.bfloat16),
            jnp.zeros((n_micro, n_rows, n_seq, n_hidden), jnp.float32),
        )

        def fwd_step(step_idx, loop_state):
            incoming, saved_all, y_store = loop_state
            mb_index = step_idx - stage_idx
            is_valid = (mb_index >= 0) & (mb_index < n_micro)
            mb_slot = jnp.clip(mb_index, 0, n_micro - 1)
            first_in = lax.dynamic_index_in_dim(acts_in, jnp.minimum(step_idx, n_micro - 1), 0, keepdims=False)
            layer_in = jnp.where(stage_idx == 0, first_in, incoming)

            def run_layer(held_bufs):
                saved_now, y_now = held_bufs
                y_act, saved = layer_forward(weights, layer_in)
                saved_now = tuple(lax.dynamic_update_index_in_dim(buf_all, buf_new, mb_slot, 0) for buf_all, buf_new in zip(saved_now, saved))
                return y_act, saved_now, lax.dynamic_update_index_in_dim(y_now, y_act, mb_slot, 0)

            def skip_layer(held_bufs):
                return jnp.zeros(mb_shape, jnp.bfloat16), held_bufs[0], held_bufs[1]

            y_act, saved_all, y_store = lax.cond(is_valid, run_layer, skip_layer, (saved_all, y_store))
            return lax.ppermute(y_act, 'pp', fwd_pairs), saved_all, y_store

        fwd_init = (jnp.zeros(mb_shape, jnp.bfloat16), saved_init, jnp.zeros(acts_in.shape, jnp.bfloat16))
        unused_in, saved_all, y_store = lax.fori_loop(0, n_steps, fwd_step, fwd_init)

        def bwd_step(step_idx, loop_state):
            incoming, grad_acc, dx_store = loop_state
            offset = step_idx - (last_stage - stage_idx)
            is_valid = (offset >= 0) & (offset < n_micro)
            mb_slot = jnp.clip(n_micro - 1 - offset, 0, n_micro - 1)
            top_ct = lax.dynamic_index_in_dim(cotangent, jnp.clip(n_micro - 1 - step_idx, 0, n_micro - 1), 0, keepdims=False)
            layer_ct = jnp.where(stage_idx == last_stage, top_ct, incoming)

            def run_back(held_bufs):
                grad_now, dx_now = held_bufs
                saved = tuple(lax.dynamic_index_in_dim(buf_all, mb_slot, 0, keepdims=False) for buf_all in saved_all)
                grad_x, w_grads = layer_backward(weights, saved, layer_ct)
                grad_now = tuple(acc_old + acc_new for acc_old, acc_new in zip(grad_now, w_grads))
                return grad_x, grad_now, lax.dynamic_update_index_in_dim(dx_now, grad_x, mb_slot, 0)

            def skip_back(held_bufs):
                return jnp.zeros(mb_shape, jnp.bfloat16), held_bufs[0], held_bufs[1]

            grad_x, grad_acc, dx_store = lax.cond(is_valid, run_back, skip_back, (grad_acc, dx_store))
            return lax.ppermute(grad_x, 'pp', bwd_pairs), grad_acc, dx_store

        grad_zero = tuple(jnp.zeros(tensor.shape, jnp.float32) for tensor in weights)
        bwd_init = (jnp.zeros(mb_shape, jnp.bfloat16), grad_zero, jnp.zeros(acts_in.shape, jnp.bfloat16))
        unused_ct, grad_acc, dx_store = lax.fori_loop(0, n_steps, bwd_step, bwd_init)
        acts_out = lax.psum(jnp.where(stage_idx == last_stage, y_store, jnp.zeros_like(y_store)), 'pp')
        grad_in = lax.psum(jnp.where(stage_idx == 0, dx_store, jnp.zeros_like(dx_store)), 'pp')
        return (acts_out, grad_in) + tuple(acc_sum[None] for acc_sum in grad_acc)

    return jax.shard_map(stage_body, mesh=mesh, in_specs=(act_spec, act_spec) + param_specs, out_specs=(act_spec, act_spec) + grad_specs, check_vma=False)
```

profile of v0, /device:TPU:113, one launch (start us, length us, event | category | flops | bytes accessed | tf_op | source)
XLA Modules:
  0.0 5279.6 jit_solution(9542383549847491413)
XLA Ops:
  15.3 46.5 broadcast_in_dim.180
  61.8 23.6 broadcast_in_dim.178
  85.4 18.4 broadcast_in_dim.177
  132.7 1380.2 %while.69 = (s32[]{:T(128)}, bf16[4,192,768]{2,1,0:T(8,128)(2,1)S(1)}, bf16[16,4,192,768]{3,2,1,0:T(8,128)(2,1)}, bf16[16,4,192,2304]{3,2,1,0:T(8,128)(2,1)}, bf...) while((s32[]{:T(128)}, ...), condition=%wide.region_9.10_spmd, body=%wide.region_0.9_spmd.sunk | while | flops 11388370944 | bytes 178891760 | solution.py:129
  137.5 50.7 collective-permute-done
  188.2 51.0 conditional.4
  254.2 51.1 conditional.4
  322.7 51.0 conditional.4
  391.4 51.0 conditional.4
  460.0 51.0 conditional.4
  528.6 50.9 conditional.4
  597.1 50.9 conditional.4
  665.6 50.9 conditional.4
  734.0 51.0 conditional.4
  802.5 51.1 conditional.4
  871.0 50.9 conditional.4
  939.6 51.0 conditional.4
  1008.1 50.9 conditional.4
  1076.7 51.1 conditional.4
  1145.1 51.1 conditional.4
  1213.8 50.9 conditional.4
  1282.5 55.2 %collective-permute-start = (bf16[4,192,768]{2,1,0:T(8,128)(2,1)S(1)}, bf16[4,192,768]{2,1,0:T(8,128)(2,1)S(1)}, u32[]{:S(2)}, u32[]{:S(2)}) collective-permute-start(bf16[4,192,768]{2,1,0:T(8,128)(2,1)S(1)} %get-tuple-element.2417), channel_id=1, source_target_pairs={{0,1},{1,2},{2,3},{3,4},{4,5},{5,6},{6,7},{8,9},{9,10},{10,11},{11... | collective-permute-start | bytes 3538952 | tf_op jit(solution)/shard_map/while/body/eval_jaxpr/ppermute | solution.py:126
  1368.6 29.3 collective-permute-start
  1428.8 53.1 %collective-permute-start = (bf16[4,192,768]{2,1,0:T(8,128)(2,1)S(1)}, bf16[4,192,768]{2,1,0:T(8,128)(2,1)S(1)}, u32[]{:S(2)}, u32[]{:S(2)}) collective-permute-start(bf16[4,192,768]{2,1,0:T(8,128)(2,1)S(1)} %get-tuple-element.2417), channel_id=1, source_target_pairs={{0,1},{1,2},{2,3},{3,4},{4,5},{5,6},{6,7},{8,9},{9,10},{10,11},{11... | collective-permute-start | bytes 3538952 | tf_op jit(solution)/shard_map/while/body/eval_jaxpr/ppermute | solution.py:126
  1512.9 81.5 %copy.50 = bf16[16,4,192,2304]{2,3,1,0:T(8,128)(2,1)} copy(bf16[16,4,192,2304]{3,2,1,0:T(8,128)(2,1)} %get-tuple-element.1918) | data formatting | bytes 113246208 | tf_op jit(solution)/shard_map/while | solution.py:154
  1594.5 21.0 copy.51
  1636.7 3218.8 %while.70 = (s32[]{:T(128)}, bf16[4,192,768]{2,1,0:T(8,128)(2,1)S(1)}, f32[768]{0:T(1024)S(1)}, f32[768]{0:T(1024)S(1)}, f32[768,2304]{1,0:T(8,128)}, /*index=5*...) while((s32[]{:T(128)}, ...), condition=%wide.region_31.32_spmd, body=%wide.region_11.31_spmd.sunk | while | flops 22827401216 | bytes 430544288 | solution.py:154
  1647.7 41.3 collective-permute-done.1
  1692.2 15.6 collective-permute-done.1
  1710.9 64.9 %collective-permute-done.1 = bf16[4,192,768]{2,1,0:T(8,128)(2,1)S(1)} collective-permute-done((bf16[4,192,768]{2,1,0:T(8,128)(2,1)}, bf16[4,192,768]{2,1,0:T(8,128)(2,1)S(1)}, u32[]{:S(2)}, u32[]{:S(2)}) %collective-permute-start.1) | collective-permute-done | bytes 1179680 | tf_op jit(solution)/shard_map/while/body/eval_jaxpr/ppermute | solution.py:150
  1778.9 15.6 collective-permute-done.1
  1797.6 41.1 collective-permute-done.1
  1841.8 703.2 %collective-permute-done.1 = bf16[4,192,768]{2,1,0:T(8,128)(2,1)S(1)} collective-permute-done((bf16[4,192,768]{2,1,0:T(8,128)(2,1)}, bf16[4,192,768]{2,1,0:T(8,128)(2,1)S(1)}, u32[]{:S(2)}, u32[]{:S(2)}) %collective-permute-start.1) | collective-permute-done | bytes 1179680 | tf_op jit(solution)/shard_map/while/body/eval_jaxpr/ppermute | solution.py:150
  2545.0 119.2 %conditional.5 = (bf16[4,192,768]{2,1,0:T(8,128)(2,1)}, f32[768]{0:T(1024)S(1)}, f32[768]{0:T(1024)S(1)}, f32[768,2304]{1,0:T(8,128)}, f32[2304]{0:T(1024)S(1)},...) conditional(s32[]{:T(128)} %convert_element_type.605, ...), branch_computations={%region_12.12_spmd, %region_13.30_spmd} | conditional | flops 22827401216 | bytes 425824960 | solution.py:149
  2666.2 17.2 collective-permute-done.1
  2683.7 119.4 %conditional.5 = (bf16[4,192,768]{2,1,0:T(8,128)(2,1)}, f32[768]{0:T(1024)S(1)}, f32[768]{0:T(1024)S(1)}, f32[768,2304]{1,0:T(8,128)}, f32[2304]{0:T(1024)S(1)},...) conditional(s32[]{:T(128)} %convert_element_type.605, ...), branch_computations={%region_12.12_spmd, %region_13.30_spmd} | conditional | flops 22827401216 | bytes 425824960 | solution.py:149
  2805.0 17.5 collective-permute-done.1
  2822.9 119.6 %conditional.5 = (bf16[4,192,768]{2,1,0:T(8,128)(2,1)}, f32[768]{0:T(1024)S(1)}, f32[768]{0:T(1024)S(1)}, f32[768,2304]{1,0:T(8,128)}, f32[2304]{0:T(1024)S(1)},...) conditional(s32[]{:T(128)} %convert_element_type.605, ...), branch_computations={%region_12.12_spmd, %region_13.30_spmd} | conditional | flops 22827401216 | bytes 425824960 | solution.py:149
  2944.5 15.6 collective-permute-done.1
  2960.3 119.0 %conditional.5 = (bf16[4,192,768]{2,1,0:T(8,128)(2,1)}, f32[768]{0:T(1024)S(1)}, f32[768]{0:T(1024)S(1)}, f32[768,2304]{1,0:T(8,128)}, f32[2304]{0:T(1024)S(1)},...) conditional(s32[]{:T(128)} %convert_element_type.605, ...), branch_computations={%region_12.12_spmd, %region_13.30_spmd} | conditional | flops 22827401216 | bytes 425824960 | solution.py:149
  3081.2 15.6 collective-permute-done.1
  3097.1 119.2 %conditional.5 = (bf16[4,192,768]{2,1,0:T(8,128)(2,1)}, f32[768]{0:T(1024)S(1)}, f32[768]{0:T(1024)S(1)}, f32[768,2304]{1,0:T(8,128)}, f32[2304]{0:T(1024)S(1)},...) conditional(s32[]{:T(128)} %convert_element_type.605, ...), branch_computations={%region_12.12_spmd, %region_13.30_spmd} | conditional | flops 22827401216 | bytes 425824960 | solution.py:149
  3218.2 15.6 collective-permute-done.1
  3234.3 119.3 %conditional.5 = (bf16[4,192,768]{2,1,0:T(8,128)(2,1)}, f32[768]{0:T(1024)S(1)}, f32[768]{0:T(1024)S(1)}, f32[768,2304]{1,0:T(8,128)}, f32[2304]{0:T(1024)S(1)},...) conditional(s32[]{:T(128)} %convert_element_type.605, ...), branch_computations={%region_12.12_spmd, %region_13.30_spmd} | conditional | flops 22827401216 | bytes 425824960 | solution.py:149
  3355.6 15.6 collective-permute-done.1
  3371.3 119.2 %conditional.5 = (bf16[4,192,768]{2,1,0:T(8,128)(2,1)}, f32[768]{0:T(1024)S(1)}, f32[768]{0:T(1024)S(1)}, f32[768,2304]{1,0:T(8,128)}, f32[2304]{0:T(1024)S(1)},...) conditional(s32[]{:T(128)} %convert_element_type.605, ...), branch_computations={%region_12.12_spmd, %region_13.30_spmd} | conditional | flops 22827401216 | bytes 425824960 | solution.py:149
  3492.5 15.6 collective-permute-done.1
  3508.3 119.1 %conditional.5 = (bf16[4,192,768]{2,1,0:T(8,128)(2,1)}, f32[768]{0:T(1024)S(1)}, f32[768]{0:T(1024)S(1)}, f32[768,2304]{1,0:T(8,128)}, f32[2304]{0:T(1024)S(1)},...) conditional(s32[]{:T(128)} %convert_element_type.605, ...), branch_computations={%region_12.12_spmd, %region_13.30_spmd} | conditional | flops 22827401216 | bytes 425824960 | solution.py:149
  3629.4 15.6 collective-permute-done.1
  3645.5 119.6 %conditional.5 = (bf16[4,192,768]{2,1,0:T(8,128)(2,1)}, f32[768]{0:T(1024)S(1)}, f32[768]{0:T(1024)S(1)}, f32[768,2304]{1,0:T(8,128)}, f32[2304]{0:T(1024)S(1)},...) conditional(s32[]{:T(128)} %convert_element_type.605, ...), branch_computations={%region_12.12_spmd, %region_13.30_spmd} | conditional | flops 22827401216 | bytes 425824960 | solution.py:149
  3767.0 15.6 collective-permute-done.1
  3782.8 119.5 %conditional.5 = (bf16[4,192,768]{2,1,0:T(8,128)(2,1)}, f32[768]{0:T(1024)S(1)}, f32[768]{0:T(1024)S(1)}, f32[768,2304]{1,0:T(8,128)}, f32[2304]{0:T(1024)S(1)},...) conditional(s32[]{:T(128)} %convert_element_type.605, ...), branch_computations={%region_12.12_spmd, %region_13.30_spmd} | conditional | flops 22827401216 | bytes 425824960 | solution.py:149
  3904.2 15.6 collective-permute-done.1
  3920.1 119.3 %conditional.5 = (bf16[4,192,768]{2,1,0:T(8,128)(2,1)}, f32[768]{0:T(1024)S(1)}, f32[768]{0:T(1024)S(1)}, f32[768,2304]{1,0:T(8,128)}, f32[2304]{0:T(1024)S(1)},...) conditional(s32[]{:T(128)} %convert_element_type.605, ...), branch_computations={%region_12.12_spmd, %region_13.30_spmd} | conditional | flops 22827401216 | bytes 425824960 | solution.py:149
  4041.3 15.6 collective-permute-done.1
  4057.4 119.2 %conditional.5 = (bf16[4,192,768]{2,1,0:T(8,128)(2,1)}, f32[768]{0:T(1024)S(1)}, f32[768]{0:T(1024)S(1)}, f32[768,2304]{1,0:T(8,128)}, f32[2304]{0:T(1024)S(1)},...) conditional(s32[]{:T(128)} %convert_element_type.605, ...), branch_computations={%region_12.12_spmd, %region_13.30_spmd} | conditional | flops 22827401216 | bytes 425824960 | solution.py:149
  4178.5 15.6 collective-permute-done.1
  4194.3 119.4 %conditional.5 = (bf16[4,192,768]{2,1,0:T(8,128)(2,1)}, f32[768]{0:T(1024)S(1)}, f32[768]{0:T(1024)S(1)}, f32[768,2304]{1,0:T(8,128)}, f32[2304]{0:T(1024)S(1)},...) conditional(s32[]{:T(128)} %convert_element_type.605, ...), branch_computations={%region_12.12_spmd, %region_13.30_spmd} | conditional | flops 22827401216 | bytes 425824960 | solution.py:149
  4331.5 119.6 %conditional.5 = (bf16[4,192,768]{2,1,0:T(8,128)(2,1)}, f32[768]{0:T(1024)S(1)}, f32[768]{0:T(1024)S(1)}, f32[768,2304]{1,0:T(8,128)}, f32[2304]{0:T(1024)S(1)},...) conditional(s32[]{:T(128)} %convert_element_type.605, ...), branch_computations={%region_12.12_spmd, %region_13.30_spmd} | conditional | flops 22827401216 | bytes 425824960 | solution.py:149
  4469.2 119.4 %conditional.5 = (bf16[4,192,768]{2,1,0:T(8,128)(2,1)}, f32[768]{0:T(1024)S(1)}, f32[768]{0:T(1024)S(1)}, f32[768,2304]{1,0:T(8,128)}, f32[2304]{0:T(1024)S(1)},...) conditional(s32[]{:T(128)} %convert_element_type.605, ...), branch_computations={%region_12.12_spmd, %region_13.30_spmd} | conditional | flops 22827401216 | bytes 425824960 | solution.py:149
  4606.3 119.2 %conditional.5 = (bf16[4,192,768]{2,1,0:T(8,128)(2,1)}, f32[768]{0:T(1024)S(1)}, f32[768]{0:T(1024)S(1)}, f32[768,2304]{1,0:T(8,128)}, f32[2304]{0:T(1024)S(1)},...) conditional(s32[]{:T(128)} %convert_element_type.605, ...), branch_computations={%region_12.12_spmd, %region_13.30_spmd} | conditional | flops 22827401216 | bytes 425824960 | solution.py:149
  4750.9 100.7 %collective-permute-start.1 = (bf16[4,192,768]{2,1,0:T(8,128)(2,1)}, bf16[4,192,768]{2,1,0:T(8,128)(2,1)S(1)}, u32[]{:S(2)}, u32[]{:S(2)}) collective-permute-start(bf16[4,192,768]{2,1,0:T(8,128)(2,1)} %get-tuple-element.2457), channel_id=1, source_target_pairs={{1,0},{2,1},{3,2},{4,3},{5,4},{6,5},{7,6},{9,8},{10,9},{11,10},{12... | collective-permute-start | bytes 3538952 | tf_op jit(solution)/shard_map/while/body/eval_jaxpr/ppermute | solution.py:150
  4872.3 374.0 %all-reduce.3.cloned.1.call-done = (bf16[16,4,192,768]{3,2,1,0:T(8,128)(2,1)}, bf16[16,4,192,768]{3,2,1,0:T(8,128)(2,1)}) async-done(((bf16[16,4,192,768]{3,2,1,0:T(8,128)(2,1)}, bf16[16,4,192,768]{3,2,1,0:T(8,128)(2,1)}), (bf16[16,4,192,768]{3,2,1,0:T(8,128)(2,1)}, bf16[16,4,192,768]{3,2,1,0:T(8,128)(2,1)})) %all-reduce.3.cloned.1.call-update) | async-done | bytes 37748752 | tf_op jit(solution)/shard_map/psum | solution.py:155
  5246.3 18.2 copy.193
  (2155 shorter events, 3306.2 us)
Async XLA Ops:
  7.2 5239.1 %all-reduce.3.cloned.1.call-start = ((), (), s32[]{:S(2)}) async-start(), calls=%async_computation | async-start | bytes 75497472 | tf_op jit(solution)/shard_map/psum | solution.py:155
  132.9 55.3 %collective-permute-start = (bf16[4,192,768]{2,1,0:T(8,128)(2,1)S(1)}, bf16[4,192,768]{2,1,0:T(8,128)(2,1)S(1)}, u32[]{:S(2)}, u32[]{:S(2)}) collective-permute-start(bf16[4,192,768]{2,1,0:T(8,128)(2,1)S(1)} %get-tuple-element.2417), channel_id=1, source_target_pairs={{0,1},{1,2},{2,3},{3,4},{4,5},{5,6},{6,7},{8,9},{9,10},{10,11},{11... | collective-permute-start | bytes 3538952 | tf_op jit(solution)/shard_map/while/body/eval_jaxpr/ppermute | solution.py:126
  239.2 15.1 collective-permute-start
  305.3 17.4 collective-permute-start
  373.8 17.6 collective-permute-start
  442.4 17.6 collective-permute-start
  511.0 17.5 collective-permute-start
  579.4 17.7 collective-permute-start
  648.0 17.5 collective-permute-start
  716.5 17.5 collective-permute-start
  785.0 17.5 collective-permute-start
  853.6 17.4 collective-permute-start
  922.0 17.7 collective-permute-start
  990.6 17.5 collective-permute-start
  1059.0 17.6 collective-permute-start
  1127.8 17.4 collective-permute-start
  1196.2 17.6 collective-permute-start
  1264.7 17.7 collective-permute-start
  1282.5 68.4 %collective-permute-start = (bf16[4,192,768]{2,1,0:T(8,128)(2,1)S(1)}, bf16[4,192,768]{2,1,0:T(8,128)(2,1)S(1)}, u32[]{:S(2)}, u32[]{:S(2)}) collective-permute-start(bf16[4,192,768]{2,1,0:T(8,128)(2,1)S(1)} %get-tuple-element.2417), channel_id=1, source_target_pairs={{0,1},{1,2},{2,3},{3,4},{4,5},{5,6},{6,7},{8,9},{9,10},{10,11},{11... | collective-permute-start | bytes 3538952 | tf_op jit(solution)/shard_map/while/body/eval_jaxpr/ppermute | solution.py:126
  1350.9 17.6 collective-permute-start
  1368.6 42.5 collective-permute-start
  1411.2 17.6 collective-permute-start
  1428.8 66.3 %collective-permute-start = (bf16[4,192,768]{2,1,0:T(8,128)(2,1)S(1)}, bf16[4,192,768]{2,1,0:T(8,128)(2,1)S(1)}, u32[]{:S(2)}, u32[]{:S(2)}) collective-permute-start(bf16[4,192,768]{2,1,0:T(8,128)(2,1)S(1)} %get-tuple-element.2417), channel_id=1, source_target_pairs={{0,1},{1,2},{2,3},{3,4},{4,5},{5,6},{6,7},{8,9},{9,10},{10,11},{11... | collective-permute-start | bytes 3538952 | tf_op jit(solution)/shard_map/while/body/eval_jaxpr/ppermute | solution.py:126
  1495.2 17.6 collective-permute-start
  1645.7 43.2 collective-permute-start.1
  1690.3 17.5 collective-permute-start.1
  1709.0 66.8 %collective-permute-start.1 = (bf16[4,192,768]{2,1,0:T(8,128)(2,1)}, bf16[4,192,768]{2,1,0:T(8,128)(2,1)S(1)}, u32[]{:S(2)}, u32[]{:S(2)}) collective-permute-start(bf16[4,192,768]{2,1,0:T(8,128)(2,1)} %get-tuple-element.2457), channel_id=1, source_target_pairs={{1,0},{2,1},{3,2},{4,3},{5,4},{6,5},{7,6},{9,8},{10,9},{11,10},{12... | collective-permute-start | bytes 3538952 | tf_op jit(solution)/shard_map/while/body/eval_jaxpr/ppermute | solution.py:150
  1776.9 17.5 collective-permute-start.1
  1795.6 43.1 collective-permute-start.1
  1839.9 705.2 %collective-permute-start.1 = (bf16[4,192,768]{2,1,0:T(8,128)(2,1)}, bf16[4,192,768]{2,1,0:T(8,128)(2,1)S(1)}, u32[]{:S(2)}, u32[]{:S(2)}) collective-permute-start(bf16[4,192,768]{2,1,0:T(8,128)(2,1)} %get-tuple-element.2457), channel_id=1, source_target_pairs={{1,0},{2,1},{3,2},{4,3},{5,4},{6,5},{7,6},{9,8},{10,9},{11,10},{12... | collective-permute-start | bytes 3538952 | tf_op jit(solution)/shard_map/while/body/eval_jaxpr/ppermute | solution.py:150
  2633.3 18.2 slice-start.2
  2664.2 19.1 collective-permute-start.1
  2772.1 18.2 slice-start.2
  2803.0 19.5 collective-permute-start.1
  2911.4 18.2 slice-start.2
  2942.6 17.6 collective-permute-start.1
  3048.4 18.2 slice-start.2
  3079.3 17.6 collective-permute-start.1
  3185.3 18.2 slice-start.2
  3216.3 17.6 collective-permute-start.1
  3322.5 18.2 slice-start.2
  3353.6 17.6 collective-permute-start.1
  3459.6 18.2 slice-start.2
  3490.5 17.6 collective-permute-start.1
  3596.5 18.2 slice-start.2
  3627.4 17.6 collective-permute-start.1
  3733.9 18.2 slice-start.1
  3733.9 18.2 slice-start.2
  3765.0 17.6 collective-permute-start.1
  3871.4 18.2 slice-start.2
  3902.3 17.6 collective-permute-start.1
  4008.4 18.2 slice-start.2
  4039.4 17.6 collective-permute-start.1
  4145.4 18.2 slice-start.2
  4176.5 17.6 collective-permute-start.1
  4282.8 18.2 slice-start.2
  4313.7 17.6 collective-permute-start.1
  4420.1 18.2 slice-start.2
  4451.1 17.6 collective-permute-start.1
  4557.4 18.2 slice-start.2
  4588.6 17.6 collective-permute-start.1
  4725.5 17.6 collective-permute-start.1
  4750.9 103.1 %collective-permute-start.1 = (bf16[4,192,768]{2,1,0:T(8,128)(2,1)}, bf16[4,192,768]{2,1,0:T(8,128)(2,1)S(1)}, u32[]{:S(2)}, u32[]{:S(2)}) collective-permute-start(bf16[4,192,768]{2,1,0:T(8,128)(2,1)} %get-tuple-element.2457), channel_id=1, source_target_pairs={{1,0},{2,1},{3,2},{4,3},{5,4},{6,5},{7,6},{9,8},{10,9},{11,10},{12... | collective-permute-start | bytes 3538952 | tf_op jit(solution)/shard_map/while/body/eval_jaxpr/ppermute | solution.py:150
  5246.3 19.0 copy-start.5
  (417 other events, 2711.8 us)
Sparse Core Ops, SparseCore 0:
  4868.3 377.9 all-reduce.2
where the time goes:
time: 5300 us; the launch traced here: 5280 us
  matrix products  1880 us (35%)
  waiting for transfers between devices  1850 us (35%)
  local copies, waits for them, and re-layouts  569 us (11%)
  other arithmetic  564 us (11%)
  starting transfers between devices  368 us (7%)
    ppermute x23, waiting for transfers between devices, bwd_step(): return (lax.ppermute(grad_x, 'pp', bwd_pairs), grad_acc, dx_store)  1140 us
    psum x1, waiting for transfers between devices, stage_body(): lax.psum(jnp.where(stage_idx == last_stage, y_store, jnp.zeros_like(y_sto...  374 us
    ppermute x23, waiting for transfers between devices, fwd_step(): return (lax.ppermute(y_act, 'pp', fwd_pairs), saved_all, y_store)  339 us
    ppermute x23, starting transfers between devices, fwd_step(): return (lax.ppermute(y_act, 'pp', fwd_pairs), saved_all, y_store)  224 us
    dot_general x16, matrix products, layer_backward(): jnp.einsum('bsd,bsf->df', h_two_f.astype(jnp.bfloat16), grad_pre_bf, pref...  215 us
    dot_general x16, matrix products, layer_backward(): jnp.einsum('bsd,fd->bsf', grad_y, w_down, preferred_element_type=jnp.floa...  187 us
    dot_general x16, matrix products, layer_backward(): jnp.einsum('bhqk,bqhd->bkhd', grad_scores, qkv_heads[:, :, 0], preferred_...  185 us
    dot_general x16, matrix products, layer_backward(): jnp.einsum('bhqk,bkhd->bqhd', grad_scores, qkv_heads[:, :, 1], preferred_...  182 us
  transfers between devices with their start and end apart: 47, of which 47 were waited for; matrix products, arithmetic and copies ran while one was open for 0% of the time, Pallas kernels for 0%

commit v1 on v0

v1 whole, which is shorter than its diff:
```python
import functools

import jax
import jax.numpy as jnp
from jax import lax
from jax.experimental import pallas as pl
from jax.experimental.pallas import tpu as pltpu
from jax.sharding import PartitionSpec as P

LN_EPS = 1e-5
PARAM_RANKS = (2, 2, 3, 2, 4, 2, 2, 2, 3, 2, 3, 2)
F32, BF16 = jnp.float32, jnp.bfloat16
PAIR = 128


def normalize(x_wide):
    mean_val = jnp.mean(x_wide, axis=-1, keepdims=True)
    centered = x_wide - mean_val
    variance = jnp.mean(centered * centered, axis=-1, keepdims=True)
    inv_std = lax.rsqrt(variance + LN_EPS)
    return centered * inv_std, inv_std


def normalize_back(grad_h, gain, x_hat, inv_std):
    grad_hat = grad_h * gain
    mean_grad = jnp.mean(grad_hat, axis=-1, keepdims=True)
    mean_dot = jnp.mean(grad_hat * x_hat, axis=-1, keepdims=True)
    return inv_std * (grad_hat - mean_grad - x_hat * mean_dot)


def gelu_tanh(pre_act):
    return jax.nn.gelu(pre_act, approximate=True)


def mat(lhs, rhs, lhs_dim=1, rhs_dim=0):
    return lax.dot_general(lhs, rhs, (((lhs_dim,), (rhs_dim,)), ((), ())), preferred_element_type=F32)


def head_probs(q_pair, k_pair, in_head, causal, scale):
    q_head = jnp.where(in_head, q_pair, jnp.zeros_like(q_pair))
    scores = jnp.where(causal, mat(q_head, k_pair, 1, 1) * scale, -1e30)
    exps = jnp.exp(scores - jnp.max(scores, axis=-1, keepdims=True))
    return (exps * (1.0 / jnp.sum(exps, axis=-1, keepdims=True))).astype(BF16)


def masks(n_seq, head_dim):
    lanes = lax.broadcasted_iota(jnp.int32, (n_seq, PAIR), 1)
    causal = lax.broadcasted_iota(jnp.int32, (n_seq, n_seq), 0) >= lax.broadcasted_iota(jnp.int32, (n_seq, n_seq), 1)
    return (lanes < head_dim, lanes >= head_dim), causal


def attn_fwd_kernel(head_dim, place, qkv_ref, o_old, o_ref):
    n_seq, width = o_ref.shape[2], o_ref.shape[3]
    in_heads, causal = masks(n_seq, head_dim)
    for col in range(0, width, PAIR):
        q_pair, k_pair, v_pair = (qkv_ref[0, 0, :, part * width + col:part * width + col + PAIR] for part in range(3))
        mixes = [mat(head_probs(q_pair, k_pair, in_head, causal, head_dim ** -0.5), v_pair) for in_head in in_heads]
        o_ref[0, 0, :, col:col + PAIR] = jnp.where(in_heads[0], mixes[0], mixes[1]).astype(BF16)


def attn_bwd_kernel(head_dim, place, qkv_ref, go_ref, g_old, g_ref):
    n_seq, width = go_ref.shape[1], go_ref.shape[2]
    in_heads, _ = masks(n_seq, head_dim)
    causal = lax.broadcasted_iota(jnp.int32, (n_seq, n_seq), 0) <= lax.broadcasted_iota(jnp.int32, (n_seq, n_seq), 1)
    scale = head_dim ** -0.5
    for col in range(0, width, PAIR):
        q_pair, k_pair, v_pair = (qkv_ref[0, 0, :, part * width + col:part * width + col + PAIR] for part in range(3))
        go_pair = go_ref[0, :, col:col + PAIR]
        grads = []
        for in_head in in_heads:
            q_head = jnp.where(in_head, q_pair, jnp.zeros_like(q_pair))
            go_head = jnp.where(in_head, go_pair, jnp.zeros_like(go_pair))
            scores = jnp.where(causal, mat(k_pair, q_head, 1, 1) * scale, -1e30)
            exps = jnp.exp(scores - jnp.max(scores, axis=0, keepdims=True))
            probs = (exps * (1.0 / jnp.sum(exps, axis=0, keepdims=True))).astype(BF16)
            grad_probs = mat(v_pair, go_head, 1, 1).astype(BF16).astype(F32)
            wide = probs.astype(F32)
            row_dot = jnp.sum(grad_probs * wide, axis=0, keepdims=True)
            grad_scores = (wide * (grad_probs - row_dot) * scale).astype(BF16)
            grads.append((mat(grad_scores, k_pair, 0, 0), mat(grad_scores, q_pair), mat(probs, go_pair)))
        for part in range(3):
            g_ref[0, 0, :, part * width + col:part * width + col + PAIR] = jnp.where(in_heads[0], grads[0][part], grads[1][part]).astype(BF16)


def attn_cost(n_rows, n_seq, width, dots):
    return pl.CostEstimate(flops=dots * 8 * n_rows * n_seq * n_seq * width, bytes_accessed=n_rows * n_seq * width * 14, transcendentals=0)


def attn_fwd(place, qkv_all, o_all, n_rows, head_dim):
    n_seq, width = o_all.shape[2:]
    spec = lambda cols: pl.BlockSpec((1, 1, n_seq, cols), lambda row, place: (place[0], place[1] + row, 0, 0))
    return pl.pallas_call(
        functools.partial(attn_fwd_kernel, head_dim),
        grid_spec=pltpu.PrefetchScalarGridSpec(
            num_scalar_prefetch=1, grid=(n_rows,),
            in_specs=[spec(3 * width), pl.BlockSpec(memory_space=pl.ANY)], out_specs=spec(width)),
        out_shape=jax.ShapeDtypeStruct(o_all.shape, BF16), input_output_aliases={2: 0},
        cost_estimate=attn_cost(n_rows, n_seq, width, 2), name="attn_fwd")(place, qkv_all, o_all)


def attn_bwd(place, qkv_all, grad_mix, g_all, head_dim):
    n_rows, n_seq, width = grad_mix.shape
    spec = lambda cols: pl.BlockSpec((1, 1, n_seq, cols), lambda row, place: (place[0], place[1] + row, 0, 0))
    return pl.pallas_call(
        functools.partial(attn_bwd_kernel, head_dim),
        grid_spec=pltpu.PrefetchScalarGridSpec(
            num_scalar_prefetch=1, grid=(n_rows,),
            in_specs=[spec(3 * width), pl.BlockSpec((1, n_seq, width), lambda row, place: (row, 0, 0)), pl.BlockSpec(memory_space=pl.ANY)],
            out_specs=spec(3 * width)),
        out_shape=jax.ShapeDtypeStruct(g_all.shape, BF16), input_output_aliases={3: 0},
        cost_estimate=attn_cost(n_rows, n_seq, width, 5), name="attn_bwd")(place, qkv_all, grad_mix, g_all)


def blank(*shapes):
    return pl.pallas_call(lambda *refs: None, out_shape=[jax.ShapeDtypeStruct(shape, BF16) for shape in shapes],
                          out_specs=[pl.BlockSpec(memory_space=pl.ANY)] * len(shapes), name="blank")()


def put(buf, value, mb, row):
    value = value.reshape((1, -1) + buf.shape[2:])
    return lax.dynamic_update_slice(buf, value, (mb, row, 0, 0))


def take(buf, mb, row, n_rows):
    return lax.dynamic_slice(buf, (mb, row, 0, 0), (1, n_rows) + buf.shape[2:]).reshape((-1,) + buf.shape[3:])


def half_forward(weights, x_act, bufs, mb, row, n_rows, head_dim):
    g_one, s_one, w_qkv, b_qkv, w_proj, b_proj, g_two, s_two, w_up, b_up, w_down, b_down = weights
    x_all, qkv_all, o_all, mid_all, y_all = bufs
    x_wide = x_act.astype(F32)
    h_one = (normalize(x_wide)[0] * g_one + s_one).astype(BF16)
    qkv_all = put(qkv_all, (mat(h_one, w_qkv) + b_qkv).astype(BF16), mb, row)
    o_all = attn_fwd(jnp.stack([mb, jnp.int32(row)]), qkv_all, o_all, n_rows, head_dim)
    x_mid = (x_wide + mat(take(o_all, mb, row, n_rows), w_proj) + b_proj).astype(BF16)
    mid_wide = x_mid.astype(F32)
    h_two = (normalize(mid_wide)[0] * g_two + s_two).astype(BF16)
    hidden = lax.optimization_barrier(gelu_tanh(mat(h_two, w_up) + b_up).astype(BF16))
    y_act = (mid_wide + mat(hidden, w_down) + b_down).astype(BF16)
    return y_act, (put(x_all, x_act, mb, row), qkv_all, o_all, put(mid_all, x_mid, mb, row), put(y_all, y_act, mb, row))


def half_backward(weights, saved, grad_y, bufs, mb, row, n_rows, head_dim):
    g_one, s_one, w_qkv, b_qkv, w_proj, b_proj, g_two, s_two, w_up, b_up, w_down, b_down = weights
    x_all, qkv_all, mid_all = saved
    gy_all, a_all, gpre_all, h2_all, gmid_all, gqkv_all, h1_all, dx_all = bufs
    grad_wide = grad_y.astype(F32)
    hat_two, inv_two = normalize(take(mid_all, mb, row, n_rows).astype(F32))
    h_two = (hat_two * g_two + s_two).astype(BF16)
    grad_hidden = mat(grad_y, w_down, 1, 1).astype(BF16)
    hidden, gelu_pull = jax.vjp(gelu_tanh, mat(h_two, w_up) + b_up)
    grad_pre = gelu_pull(grad_hidden.astype(F32))[0]
    grad_pre_bf = grad_pre.astype(BF16)
    grad_h_two = mat(grad_pre_bf, w_up, 1, 1).astype(BF16).astype(F32)
    grad_mid = (grad_wide + normalize_back(grad_h_two, g_two, hat_two, inv_two)).astype(BF16)
    mid_f32 = grad_mid.astype(F32)
    grad_mix = mat(grad_mid, w_proj, 1, 1).astype(BF16)
    n_seq = gqkv_all.shape[2]
    gqkv_all = attn_bwd(jnp.stack([mb, jnp.int32(row)]), qkv_all, grad_mix.reshape(n_rows, n_seq, -1), gqkv_all, head_dim)
    grad_qkv = take(gqkv_all, mb, row, n_rows)
    hat_one, inv_one = normalize(take(x_all, mb, row, n_rows).astype(F32))
    h_one = (hat_one * g_one + s_one).astype(BF16)
    grad_h_one = mat(grad_qkv, w_qkv, 1, 1).astype(BF16).astype(F32)
    grad_x = (mid_f32 + normalize_back(grad_h_one, g_one, hat_one, inv_one)).astype(BF16)
    sums = (jnp.sum(grad_h_one * hat_one, 0), jnp.sum(grad_h_one, 0),
            jnp.sum(grad_h_two * hat_two, 0), jnp.sum(grad_h_two, 0), jnp.sum(grad_pre, 0))
    values = (grad_y, hidden.astype(BF16), grad_pre_bf, h_two, grad_mid, None, h_one, grad_x)
    bufs = tuple(gqkv_all if value is None else put(buf, value, mb, row) for buf, value in zip(bufs, values))
    return grad_x, bufs, sums


def solution(mesh):
    n_stages = mesh.shape['pp']
    last_stage = n_stages - 1
    fwd_pairs = [(source, source + 1) for source in range(n_stages - 1)]
    bwd_pairs = [(source + 1, source) for source in range(n_stages - 1)]
    act_spec = P(None, 'dp', None, None)
    param_specs = tuple(P(*(('pp',) + (None,) * (rank_n - 1))) for rank_n in PARAM_RANKS)
    grad_specs = tuple(P(*((('dp', 'pp'),) + (None,) * (rank_n - 1))) for rank_n in PARAM_RANKS)

    def stage_body(acts_in, cotangent, *stacked_w):
        weights = tuple(tensor[0].astype(F32) if tensor.ndim == 2 else tensor[0] for tensor in stacked_w)
        head_dim = stacked_w[4].shape[2]
        weights = weights[:4] + (weights[4].reshape(-1, weights[4].shape[-1]),) + weights[5:]
        stage_idx = lax.axis_index('pp')
        n_micro, n_rows, n_seq, n_width = acts_in.shape
        n_hidden = stacked_w[8].shape[2]
        half = n_rows // 2
        n_steps = n_micro + n_stages - 1
        sized = lambda width: (n_micro, n_rows, n_seq, width)
        no_rows = jnp.zeros((half * n_seq, n_width), BF16)
        slabs = blank(*(sized(w) for w in (n_width, 3 * n_width, n_width, n_width, n_width)))

        def fwd_step(step_idx, loop_state):
            in_top, sent_low, bufs = loop_state
            in_low = lax.ppermute(sent_low, 'pp', fwd_pairs)
            mb = jnp.clip(step_idx - stage_idx, 0, n_micro - 1)
            first = jnp.minimum(step_idx, n_micro - 1)
            x_top = jnp.where(stage_idx == 0, take(acts_in, first, 0, half), in_top)
            y_top, bufs = half_forward(weights, x_top, bufs, mb, 0, half, head_dim)
            in_top = lax.ppermute(y_top, 'pp', fwd_pairs)
            x_low = jnp.where(stage_idx == 0, take(acts_in, first, half, half), in_low)
            y_low, bufs = half_forward(weights, x_low, bufs, mb, half, half, head_dim)
            return in_top, y_low, bufs

        _, _, saved = lax.fori_loop(0, n_steps, fwd_step, (no_rows, no_rows, tuple(slabs)))
        x_all, qkv_all, o_all, mid_all, y_all = saved
        slabs = blank(*(sized(w) for w in (n_width, n_hidden, n_hidden, n_width, n_width, 3 * n_width, n_width, n_width)))

        def bwd_step(step_idx, loop_state):
            in_top, sent_low, bufs, sums = loop_state
            in_low = lax.ppermute(sent_low, 'pp', bwd_pairs)
            offset = step_idx - (last_stage - stage_idx)
            is_valid = (offset >= 0) & (offset < n_micro)
            mb = jnp.clip(n_micro - 1 - offset, 0, n_micro - 1)
            first = jnp.clip(n_micro - 1 - step_idx, 0, n_micro - 1)
            saved_now = (x_all, qkv_all, mid_all)
            g_top = jnp.where(stage_idx == last_stage, take(cotangent, first, 0, half), in_top)
            gx_top, bufs, sums_top = half_backward(weights, saved_now, g_top, bufs, mb, 0, half, head_dim)
            in_top = lax.ppermute(gx_top, 'pp', bwd_pairs)
            g_low = jnp.where(stage_idx == last_stage, take(cotangent, first, half, half), in_low)
            gx_low, bufs, sums_low = half_backward(weights, saved_now, g_low, bufs, mb, half, half, head_dim)
            sums = tuple(old + jnp.where(is_valid, top + low, 0.0) for old, top, low in zip(sums, sums_top, sums_low))
            return in_top, gx_low, bufs, sums

        zero_sums = tuple(jnp.zeros((w,), F32) for w in (n_width, n_width, n_width, n_width, n_hidden))
        init = (no_rows, no_rows, tuple(slabs), zero_sums)
        acts_out = lax.psum(jnp.where(stage_idx == last_stage, y_all, jnp.zeros_like(y_all)), 'pp')
        _, _, bufs, sums = lax.fori_loop(0, n_steps, bwd_step, init)
        gy_all, a_all, gpre_all, h2_all, gmid_all, gqkv_all, h1_all, dx_all = bufs
        grad_in = lax.psum(jnp.where(stage_idx == 0, dx_all, jnp.zeros_like(dx_all)), 'pp')
        over_tokens = lambda lhs, rhs: mat(lhs.reshape(-1, lhs.shape[-1]), rhs.reshape(-1, rhs.shape[-1]), 0, 0)
        grad_w_qkv = over_tokens(h1_all, gqkv_all)
        grad_w_proj = over_tokens(o_all, gmid_all).reshape(stacked_w[4].shape[1:])
        grad_w_up = over_tokens(h2_all, gpre_all)
        grad_w_down = over_tokens(a_all, gy_all)
        all_rows = lambda buf: jnp.sum(buf, axis=(0, 1, 2), dtype=F32)
        grads = (sums[0], sums[1], grad_w_qkv, all_rows(gqkv_all), grad_w_proj, all_rows(gmid_all), sums[2], sums[3], grad_w_up, sums[4], grad_w_down, all_rows(gy_all))
        return (acts_out, grad_in) + tuple(acc_sum[None] for acc_sum in grads)

    return jax.shard_map(stage_body, mesh=mesh, in_specs=(act_spec, act_spec) + param_specs, out_specs=(act_spec, act_spec) + grad_specs, check_vma=False)
```

time: 5300 us -> 4590 us (0.87)
  waiting for transfers between devices: 1850 us -> 142 us
  Pallas kernels: 0 us -> 816 us
  local copies, waits for them, and re-layouts: 569 us -> 809 us
  starting transfers between devices: 368 us -> 186 us
  other arithmetic: 564 us -> 735 us
  matrix products: 1880 us -> 1810 us
    ppermute x46 -> x92, waiting for transfers between devices: 1480 us -> 48.3 us  [the longest x23 48.1 us: bwd_step(): in_top = lax.ppermute(gx_top, 'pp', bwd_pairs)]
    pallas_call x0 -> x94, Pallas kernels: none -> 816 us  [the longest x46 548 us: attn_bwd(): pl.pallas_call(functools.partial(attn_bwd_kernel, head_dim), grid_spec=pl...]
    dynamic_update_slice x16 -> x391, local copies, waits for them, and re-layouts: 17.6 us -> 456 us  [put(): return lax.dynamic_update_slice(buf, value, (mb, row, 0, 0))]
    psum x1, waiting for transfers between devices: 374 us -> 93.7 us  [stage_body(): lax.psum(jnp.where(stage_idx == last_stage, y_all, jnp.zeros_like(y_all))...]
    ppermute x46 -> x92, starting transfers between devices: 368 us -> 186 us  [the longest x23 50.9 us: fwd_step(): in_low = lax.ppermute(sent_low, 'pp', fwd_pairs)]
    convert_element_type x192 -> x74, other arithmetic: 0.67 us -> 171 us  [the longest x23 69.1 us: half_backward(): (mid_f32 + normalize_back(grad_h_one, g_one, hat_one, inv_one)).astype(BF16)]
    dynamic_slice x16 -> x138, local copies, waits for them, and re-layouts: 42.4 us -> 188 us  [take(): lax.dynamic_slice(buf, (mb, row, 0, 0), (1, n_rows) + buf.shape[2:])]
    cond x864 -> x0, local copies, waits for them, and re-layouts: 117 us -> none
where the time goes in v1:
time: 4590 us; the launch traced here: 4560 us
  matrix products  1810 us (39%)
  Pallas kernels  816 us (18%)
  local copies, waits for them, and re-layouts  809 us (18%)
  other arithmetic  735 us (16%)
  starting transfers between devices  186 us (4%)
  waiting for transfers between devices  142 us (3%)
  loops' own time  51.5 us (1%)
    dot_general x418, matrix products, mat(): lax.dot_general(lhs, rhs, (((lhs_dim,), (rhs_dim,)), ((), ())), preferred...  1810 us
    pallas_call x46, Pallas kernels, attn_bwd(): pl.pallas_call(functools.partial(attn_bwd_kernel, head_dim), grid_spec=pl...  548 us
    dynamic_update_slice x391, local copies, waits for them, and re-layouts, put(): return lax.dynamic_update_slice(buf, value, (mb, row, 0, 0))  456 us
    pallas_call x46, Pallas kernels, attn_fwd(): pl.pallas_call(functools.partial(attn_fwd_kernel, head_dim), grid_spec=pl...  268 us
    dynamic_update_slice x92, other arithmetic, put(): return lax.dynamic_update_slice(buf, value, (mb, row, 0, 0))  218 us
    dynamic_slice x138, local copies, waits for them, and re-layouts, take(): lax.dynamic_slice(buf, (mb, row, 0, 0), (1, n_rows) + buf.shape[2:])  188 us
    psum x1, waiting for transfers between devices, stage_body(): lax.psum(jnp.where(stage_idx == last_stage, y_all, jnp.zeros_like(y_all))...  93.7 us

profile of v1, /device:TPU:113, one launch (start us, length us, event | category | flops | bytes accessed | tf_op | source)
XLA Modules:
  0.0 4560.0 jit_solution(8609250515907525118)
XLA Ops:
  12.8 1273.4 %while.72 = (s32[]{:T(128)}, bf16[384,768]{1,0:T(8,128)(2,1)S(1)}, bf16[384,768]{1,0:T(8,128)(2,1)S(1)}, bf16[16,4,192,768]{3,2,1,0:T(8,128)(2,1)}, bf16[16,4,19...) while((s32[]{:T(128)}, bf16[384,768]{1,0:T(8,128)(2,1)S(1)}, ...), condition=%wide.region_9.10_spmd.clone, body=%wide.region_0.9_spmd.clone.sunk | while | flops 12730468352 | bytes 145334512 | solution.py:206
  1294.4 2852.8 %while.73 = (s32[]{:T(128)}, bf16[384,768]{1,0:T(8,128)(2,1)S(1)}, bf16[384,768]{1,0:T(8,128)(2,1)S(1)}, bf16[16,4,192,768]{3,2,1,0:T(8,128)(2,1)}, bf16[16,4,19...) while((s32[]{:T(128)}, bf16[384,768]{1,0:T(8,128)(2,1)S(1)}, ...), condition=%wide.region_38.39_spmd.clone, body=%wide.region_11.38_spmd.clone.sunk | while | flops 19150712832 | bytes 266335504 | solution.py:229
  1390.1 11.9 attn_bwd.10.g_old
  1403.6 12.0 attn_bwd.11
  1513.0 11.9 attn_bwd.10.g_old
  1526.5 12.0 attn_bwd.11
  1635.9 11.9 attn_bwd.10.g_old
  1649.4 12.0 attn_bwd.11
  1758.8 11.9 attn_bwd.10.g_old
  1772.3 12.0 attn_bwd.11
  1881.7 11.9 attn_bwd.10.g_old
  1895.2 12.0 attn_bwd.11
  2004.6 11.9 attn_bwd.10.g_old
  2018.1 12.0 attn_bwd.11
  2127.5 11.9 attn_bwd.10.g_old
  2141.0 12.0 attn_bwd.11
  2213.1 8.6 fusion.277
  2250.4 11.9 attn_bwd.10.g_old
  2263.9 11.9 attn_bwd.11
  2373.3 11.9 attn_bwd.10.g_old
  2386.9 11.9 attn_bwd.11
  2496.1 11.9 attn_bwd.10.g_old
  2509.6 11.9 attn_bwd.11
  2618.9 11.9 attn_bwd.10.g_old
  2632.4 12.0 attn_bwd.11
  2704.5 8.6 fusion.277
  2741.7 11.9 attn_bwd.10.g_old
  2755.2 11.9 attn_bwd.11
  2864.8 11.9 attn_bwd.10.g_old
  2878.2 11.9 attn_bwd.11
  2987.5 11.9 attn_bwd.10.g_old
  3001.0 11.9 attn_bwd.11
  3073.3 8.6 fusion.277
  3110.6 11.9 attn_bwd.10.g_old
  3124.1 11.9 attn_bwd.11
  3233.5 11.9 attn_bwd.10.g_old
  3247.0 11.9 attn_bwd.11
  3319.0 8.6 fusion.277
  3356.4 11.9 attn_bwd.10.g_old
  3369.8 11.9 attn_bwd.11
  3479.2 11.9 attn_bwd.10.g_old
  3492.7 11.9 attn_bwd.11
  3564.7 8.6 fusion.277
  3602.0 11.9 attn_bwd.10.g_old
  3615.5 11.9 attn_bwd.11
  3725.0 12.0 attn_bwd.10.g_old
  3738.6 11.9 attn_bwd.11
  3810.6 8.6 fusion.277
  3848.0 11.9 attn_bwd.10.g_old
  3861.5 11.9 attn_bwd.11
  3970.7 11.9 attn_bwd.10.g_old
  3984.3 11.9 attn_bwd.11
  4056.2 8.6 fusion.277
  4093.5 11.9 attn_bwd.10.g_old
  4107.0 11.9 attn_bwd.11
  4154.6 24.7 copy.32
  4190.6 9.8 convert_reduce_fusion.14
  4200.9 18.6 convert_reduce_fusion.12
  4221.6 19.5 convolution_bitcast_fusion.3
  4241.1 53.4 %convolution_bitcast_fusion.2 = f32[1,768,2304]{2,1,0:T(8,128)} fusion(bf16[16,4,192,768]{3,2,1,0:T(8,128)(2,1)} %get-tuple-element.1256, bf16[16,4,192,2304]{3,2,1,0:T(8,128)(2,1)} %get-tuple-element.1257), kind=kOutput, calls=%fused_computation.266 | convolution fusion | flops 43486543872 | bytes 82575360 | tf_op jit(solution)/shard_map/dot_general | solution.py:36
  4294.5 70.2 %convolution_bitcast_fusion = f32[1,3072,768]{2,1,0:T(8,128)} fusion(bf16[16,4,192,3072]{3,2,1,0:T(8,128)(2,1)} %get-tuple-element.1265, bf16[16,4,192,768]{3,2,1,0:T(8,128)(2,1)} %get-tuple-element.1266), kind=kOutput, calls=%fused_computation.264 | convolution fusion | flops 57982058496 | bytes 103809024 | tf_op jit(solution)/shard_map/dot_general | solution.py:36
  4364.7 68.3 %convolution_bitcast_fusion.1 = f32[1,768,3072]{2,1,0:T(8,128)} fusion(bf16[16,4,192,768]{3,2,1,0:T(8,128)(2,1)} %get-tuple-element.1262, bf16[16,4,192,3072]{3,2,1,0:T(8,128)(2,1)} %get-tuple-element.1263), kind=kOutput, calls=%fused_computation.265 | convolution fusion | flops 57982058496 | bytes 103809024 | tf_op jit(solution)/shard_map/dot_general | solution.py:36
  4433.0 93.7 %all-reduce.3.cloned.1.call-done = (bf16[16,4,192,768]{3,2,1,0:T(8,128)(2,1)}, bf16[16,4,192,768]{3,2,1,0:T(8,128)(2,1)}) async-done(((bf16[16,4,192,768]{3,2,1,0:T(8,128)(2,1)}, bf16[16,4,192,768]{3,2,1,0:T(8,128)(2,1)}), (bf16[16,4,192,768]{3,2,1,0:T(8,128)(2,1)}, bf16[16,4,192,768]{3,2,1,0:T(8,128)(2,1)})) %all-reduce.3.cloned.1.call-update) | async-done | bytes 37748752 | tf_op jit(solution)/shard_map/psum | solution.py:228
  4526.8 18.2 copy.136
  (5887 shorter events, 3508.9 us)
Async XLA Ops:
  7.2 4519.6 %all-reduce.3.cloned.1.call-start = ((), (), s32[]{:S(2)}) async-start(), calls=%async_computation | async-start | bytes 75497472 | tf_op jit(solution)/shard_map/psum | solution.py:228
  13.7 32.4 collective-permute-start.1
  41.6 29.1 collective-permute-start
  71.5 31.5 collective-permute-start.1
  98.5 29.1 collective-permute-start
  128.4 31.2 collective-permute-start.1
  155.1 29.1 collective-permute-start
  185.0 29.8 collective-permute-start.1
  240.1 29.9 collective-permute-start.1
  265.4 29.1 collective-permute-start
  295.3 29.7 collective-permute-start.1
  350.4 29.9 collective-permute-start.1
  375.8 29.0 collective-permute-start
  405.6 29.8 collective-permute-start.1
  430.8 29.1 collective-permute-start
  460.8 29.7 collective-permute-start.1
  486.0 29.0 collective-permute-start
  515.9 29.8 collective-permute-start.1
  571.0 29.9 collective-permute-start.1
  596.3 29.0 collective-permute-start
  626.2 29.8 collective-permute-start.1
  651.4 29.0 collective-permute-start
  681.3 29.7 collective-permute-start.1
  706.5 29.0 collective-permute-start
  736.3 29.8 collective-permute-start.1
  761.5 29.0 collective-permute-start
  791.4 29.7 collective-permute-start.1
  816.6 29.0 collective-permute-start
  846.5 29.7 collective-permute-start.1
  871.7 29.0 collective-permute-start
  901.6 29.8 collective-permute-start.1
  926.8 29.0 collective-permute-start
  956.6 29.8 collective-permute-start.1
  981.9 29.0 collective-permute-start
  1011.7 29.8 collective-permute-start.1
  1066.8 29.8 collective-permute-start.1
  1121.9 29.8 collective-permute-start.1
  1147.1 29.0 collective-permute-start
  1176.9 29.8 collective-permute-start.1
  1202.2 29.0 collective-permute-start
  1232.0 29.8 collective-permute-start.1
  1316.1 53.9 %collective-permute-start.2 = (bf16[384,768]{1,0:T(8,128)(2,1)}, bf16[384,768]{1,0:T(8,128)(2,1)}, u32[]{:S(2)}, u32[]{:S(2)}) collective-permute-start(bf16[384,768]{1,0:T(8,128)(2,1)} %broadcast_select_fusion.7), channel_id=1, source_target_pairs={{1,0},{2,1},{3,2},{4,3},{5,4},{6,5},{7,6},{9,8},{10,9},{11,10},{12... | collective-permute-start | bytes 1769480 | tf_op jit(solution)/shard_map/while/body/eval_jaxpr/ppermute | solution.py:212
  1439.5 53.4 %collective-permute-start.2 = (bf16[384,768]{1,0:T(8,128)(2,1)}, bf16[384,768]{1,0:T(8,128)(2,1)}, u32[]{:S(2)}, u32[]{:S(2)}) collective-permute-start(bf16[384,768]{1,0:T(8,128)(2,1)} %broadcast_select_fusion.7), channel_id=1, source_target_pairs={{1,0},{2,1},{3,2},{4,3},{5,4},{6,5},{7,6},{9,8},{10,9},{11,10},{12... | collective-permute-start | bytes 1769480 | tf_op jit(solution)/shard_map/while/body/eval_jaxpr/ppermute | solution.py:212
  1562.4 53.4 %collective-permute-start.2 = (bf16[384,768]{1,0:T(8,128)(2,1)}, bf16[384,768]{1,0:T(8,128)(2,1)}, u32[]{:S(2)}, u32[]{:S(2)}) collective-permute-start(bf16[384,768]{1,0:T(8,128)(2,1)} %broadcast_select_fusion.7), channel_id=1, source_target_pairs={{1,0},{2,1},{3,2},{4,3},{5,4},{6,5},{7,6},{9,8},{10,9},{11,10},{12... | collective-permute-start | bytes 1769480 | tf_op jit(solution)/shard_map/while/body/eval_jaxpr/ppermute | solution.py:212
  1685.3 53.4 %collective-permute-start.2 = (bf16[384,768]{1,0:T(8,128)(2,1)}, bf16[384,768]{1,0:T(8,128)(2,1)}, u32[]{:S(2)}, u32[]{:S(2)}) collective-permute-start(bf16[384,768]{1,0:T(8,128)(2,1)} %broadcast_select_fusion.7), channel_id=1, source_target_pairs={{1,0},{2,1},{3,2},{4,3},{5,4},{6,5},{7,6},{9,8},{10,9},{11,10},{12... | collective-permute-start | bytes 1769480 | tf_op jit(solution)/shard_map/while/body/eval_jaxpr/ppermute | solution.py:212
  1808.2 53.4 %collective-permute-start.2 = (bf16[384,768]{1,0:T(8,128)(2,1)}, bf16[384,768]{1,0:T(8,128)(2,1)}, u32[]{:S(2)}, u32[]{:S(2)}) collective-permute-start(bf16[384,768]{1,0:T(8,128)(2,1)} %broadcast_select_fusion.7), channel_id=1, source_target_pairs={{1,0},{2,1},{3,2},{4,3},{5,4},{6,5},{7,6},{9,8},{10,9},{11,10},{12... | collective-permute-start | bytes 1769480 | tf_op jit(solution)/shard_map/while/body/eval_jaxpr/ppermute | solution.py:212
  1931.1 53.4 %collective-permute-start.2 = (bf16[384,768]{1,0:T(8,128)(2,1)}, bf16[384,768]{1,0:T(8,128)(2,1)}, u32[]{:S(2)}, u32[]{:S(2)}) collective-permute-start(bf16[384,768]{1,0:T(8,128)(2,1)} %broadcast_select_fusion.7), channel_id=1, source_target_pairs={{1,0},{2,1},{3,2},{4,3},{5,4},{6,5},{7,6},{9,8},{10,9},{11,10},{12... | collective-permute-start | bytes 1769480 | tf_op jit(solution)/shard_map/while/body/eval_jaxpr/ppermute | solution.py:212
  2054.1 53.4 %collective-permute-start.2 = (bf16[384,768]{1,0:T(8,128)(2,1)}, bf16[384,768]{1,0:T(8,128)(2,1)}, u32[]{:S(2)}, u32[]{:S(2)}) collective-permute-start(bf16[384,768]{1,0:T(8,128)(2,1)} %broadcast_select_fusion.7), channel_id=1, source_target_pairs={{1,0},{2,1},{3,2},{4,3},{5,4},{6,5},{7,6},{9,8},{10,9},{11,10},{12... | collective-permute-start | bytes 1769480 | tf_op jit(solution)/shard_map/while/body/eval_jaxpr/ppermute | solution.py:212
  2177.0 53.3 %collective-permute-start.2 = (bf16[384,768]{1,0:T(8,128)(2,1)}, bf16[384,768]{1,0:T(8,128)(2,1)}, u32[]{:S(2)}, u32[]{:S(2)}) collective-permute-start(bf16[384,768]{1,0:T(8,128)(2,1)} %broadcast_select_fusion.7), channel_id=1, source_target_pairs={{1,0},{2,1},{3,2},{4,3},{5,4},{6,5},{7,6},{9,8},{10,9},{11,10},{12... | collective-permute-start | bytes 1769480 | tf_op jit(solution)/shard_map/while/body/eval_jaxpr/ppermute | solution.py:212
  2299.8 53.4 %collective-permute-start.2 = (bf16[384,768]{1,0:T(8,128)(2,1)}, bf16[384,768]{1,0:T(8,128)(2,1)}, u32[]{:S(2)}, u32[]{:S(2)}) collective-permute-start(bf16[384,768]{1,0:T(8,128)(2,1)} %broadcast_select_fusion.7), channel_id=1, source_target_pairs={{1,0},{2,1},{3,2},{4,3},{5,4},{6,5},{7,6},{9,8},{10,9},{11,10},{12... | collective-permute-start | bytes 1769480 | tf_op jit(solution)/shard_map/while/body/eval_jaxpr/ppermute | solution.py:212
  2422.7 53.3 %collective-permute-start.2 = (bf16[384,768]{1,0:T(8,128)(2,1)}, bf16[384,768]{1,0:T(8,128)(2,1)}, u32[]{:S(2)}, u32[]{:S(2)}) collective-permute-start(bf16[384,768]{1,0:T(8,128)(2,1)} %broadcast_select_fusion.7), channel_id=1, source_target_pairs={{1,0},{2,1},{3,2},{4,3},{5,4},{6,5},{7,6},{9,8},{10,9},{11,10},{12... | collective-permute-start | bytes 1769480 | tf_op jit(solution)/shard_map/while/body/eval_jaxpr/ppermute | solution.py:212
  2545.5 53.3 %collective-permute-start.2 = (bf16[384,768]{1,0:T(8,128)(2,1)}, bf16[384,768]{1,0:T(8,128)(2,1)}, u32[]{:S(2)}, u32[]{:S(2)}) collective-permute-start(bf16[384,768]{1,0:T(8,128)(2,1)} %broadcast_select_fusion.7), channel_id=1, source_target_pairs={{1,0},{2,1},{3,2},{4,3},{5,4},{6,5},{7,6},{9,8},{10,9},{11,10},{12... | collective-permute-start | bytes 1769480 | tf_op jit(solution)/shard_map/while/body/eval_jaxpr/ppermute | solution.py:212
  2668.4 53.2 %collective-permute-start.2 = (bf16[384,768]{1,0:T(8,128)(2,1)}, bf16[384,768]{1,0:T(8,128)(2,1)}, u32[]{:S(2)}, u32[]{:S(2)}) collective-permute-start(bf16[384,768]{1,0:T(8,128)(2,1)} %broadcast_select_fusion.7), channel_id=1, source_target_pairs={{1,0},{2,1},{3,2},{4,3},{5,4},{6,5},{7,6},{9,8},{10,9},{11,10},{12... | collective-permute-start | bytes 1769480 | tf_op jit(solution)/shard_map/while/body/eval_jaxpr/ppermute | solution.py:212
  2791.2 53.4 %collective-permute-start.2 = (bf16[384,768]{1,0:T(8,128)(2,1)}, bf16[384,768]{1,0:T(8,128)(2,1)}, u32[]{:S(2)}, u32[]{:S(2)}) collective-permute-start(bf16[384,768]{1,0:T(8,128)(2,1)} %broadcast_select_fusion.7), channel_id=1, source_target_pairs={{1,0},{2,1},{3,2},{4,3},{5,4},{6,5},{7,6},{9,8},{10,9},{11,10},{12... | collective-permute-start | bytes 1769480 | tf_op jit(solution)/shard_map/while/body/eval_jaxpr/ppermute | solution.py:212
  2914.1 53.3 %collective-permute-start.2 = (bf16[384,768]{1,0:T(8,128)(2,1)}, bf16[384,768]{1,0:T(8,128)(2,1)}, u32[]{:S(2)}, u32[]{:S(2)}) collective-permute-start(bf16[384,768]{1,0:T(8,128)(2,1)} %broadcast_select_fusion.7), channel_id=1, source_target_pairs={{1,0},{2,1},{3,2},{4,3},{5,4},{6,5},{7,6},{9,8},{10,9},{11,10},{12... | collective-permute-start | bytes 1769480 | tf_op jit(solution)/shard_map/while/body/eval_jaxpr/ppermute | solution.py:212
  3037.0 53.5 %collective-permute-start.2 = (bf16[384,768]{1,0:T(8,128)(2,1)}, bf16[384,768]{1,0:T(8,128)(2,1)}, u32[]{:S(2)}, u32[]{:S(2)}) collective-permute-start(bf16[384,768]{1,0:T(8,128)(2,1)} %broadcast_select_fusion.7), channel_id=1, source_target_pairs={{1,0},{2,1},{3,2},{4,3},{5,4},{6,5},{7,6},{9,8},{10,9},{11,10},{12... | collective-permute-start | bytes 1769480 | tf_op jit(solution)/shard_map/while/body/eval_jaxpr/ppermute | solution.py:212
  3160.0 53.4 %collective-permute-start.2 = (bf16[384,768]{1,0:T(8,128)(2,1)}, bf16[384,768]{1,0:T(8,128)(2,1)}, u32[]{:S(2)}, u32[]{:S(2)}) collective-permute-start(bf16[384,768]{1,0:T(8,128)(2,1)} %broadcast_select_fusion.7), channel_id=1, source_target_pairs={{1,0},{2,1},{3,2},{4,3},{5,4},{6,5},{7,6},{9,8},{10,9},{11,10},{12... | collective-permute-start | bytes 1769480 | tf_op jit(solution)/shard_map/while/body/eval_jaxpr/ppermute | solution.py:212
  3282.9 53.4 %collective-permute-start.2 = (bf16[384,768]{1,0:T(8,128)(2,1)}, bf16[384,768]{1,0:T(8,128)(2,1)}, u32[]{:S(2)}, u32[]{:S(2)}) collective-permute-start(bf16[384,768]{1,0:T(8,128)(2,1)} %broadcast_select_fusion.7), channel_id=1, source_target_pairs={{1,0},{2,1},{3,2},{4,3},{5,4},{6,5},{7,6},{9,8},{10,9},{11,10},{12... | collective-permute-start | bytes 1769480 | tf_op jit(solution)/shard_map/while/body/eval_jaxpr/ppermute | solution.py:212
  3405.7 53.4 %collective-permute-start.2 = (bf16[384,768]{1,0:T(8,128)(2,1)}, bf16[384,768]{1,0:T(8,128)(2,1)}, u32[]{:S(2)}, u32[]{:S(2)}) collective-permute-start(bf16[384,768]{1,0:T(8,128)(2,1)} %broadcast_select_fusion.7), channel_id=1, source_target_pairs={{1,0},{2,1},{3,2},{4,3},{5,4},{6,5},{7,6},{9,8},{10,9},{11,10},{12... | collective-permute-start | bytes 1769480 | tf_op jit(solution)/shard_map/while/body/eval_jaxpr/ppermute | solution.py:212
  3528.5 53.4 %collective-permute-start.2 = (bf16[384,768]{1,0:T(8,128)(2,1)}, bf16[384,768]{1,0:T(8,128)(2,1)}, u32[]{:S(2)}, u32[]{:S(2)}) collective-permute-start(bf16[384,768]{1,0:T(8,128)(2,1)} %broadcast_select_fusion.7), channel_id=1, source_target_pairs={{1,0},{2,1},{3,2},{4,3},{5,4},{6,5},{7,6},{9,8},{10,9},{11,10},{12... | collective-permute-start | bytes 1769480 | tf_op jit(solution)/shard_map/while/body/eval_jaxpr/ppermute | solution.py:212
  3651.5 53.4 %collective-permute-start.2 = (bf16[384,768]{1,0:T(8,128)(2,1)}, bf16[384,768]{1,0:T(8,128)(2,1)}, u32[]{:S(2)}, u32[]{:S(2)}) collective-permute-start(bf16[384,768]{1,0:T(8,128)(2,1)} %broadcast_select_fusion.7), channel_id=1, source_target_pairs={{1,0},{2,1},{3,2},{4,3},{5,4},{6,5},{7,6},{9,8},{10,9},{11,10},{12... | collective-permute-start | bytes 1769480 | tf_op jit(solution)/shard_map/while/body/eval_jaxpr/ppermute | solution.py:212
  3774.4 53.5 %collective-permute-start.2 = (bf16[384,768]{1,0:T(8,128)(2,1)}, bf16[384,768]{1,0:T(8,128)(2,1)}, u32[]{:S(2)}, u32[]{:S(2)}) collective-permute-start(bf16[384,768]{1,0:T(8,128)(2,1)} %broadcast_select_fusion.7), channel_id=1, source_target_pairs={{1,0},{2,1},{3,2},{4,3},{5,4},{6,5},{7,6},{9,8},{10,9},{11,10},{12... | collective-permute-start | bytes 1769480 | tf_op jit(solution)/shard_map/while/body/eval_jaxpr/ppermute | solution.py:212
  3897.4 53.3 %collective-permute-start.2 = (bf16[384,768]{1,0:T(8,128)(2,1)}, bf16[384,768]{1,0:T(8,128)(2,1)}, u32[]{:S(2)}, u32[]{:S(2)}) collective-permute-start(bf16[384,768]{1,0:T(8,128)(2,1)} %broadcast_select_fusion.7), channel_id=1, source_target_pairs={{1,0},{2,1},{3,2},{4,3},{5,4},{6,5},{7,6},{9,8},{10,9},{11,10},{12... | collective-permute-start | bytes 1769480 | tf_op jit(solution)/shard_map/while/body/eval_jaxpr/ppermute | solution.py:212
  4020.1 53.3 %collective-permute-start.2 = (bf16[384,768]{1,0:T(8,128)(2,1)}, bf16[384,768]{1,0:T(8,128)(2,1)}, u32[]{:S(2)}, u32[]{:S(2)}) collective-permute-start(bf16[384,768]{1,0:T(8,128)(2,1)} %broadcast_select_fusion.7), channel_id=1, source_target_pairs={{1,0},{2,1},{3,2},{4,3},{5,4},{6,5},{7,6},{9,8},{10,9},{11,10},{12... | collective-permute-start | bytes 1769480 | tf_op jit(solution)/shard_map/while/body/eval_jaxpr/ppermute | solution.py:212
  (1604 other events, 10708.9 us)
Sparse Core Ops, SparseCore 0:
  4154.7 372.0 all-reduce.2
